TPU v7x, 256 devices: a whole 4x4x8 slice. The times are simulated.
256 devices in a mesh: dp: 4 (over y), ctx: 64 (over x, z, core).
Axes of the slice: x: 4, y: 4, z: 8, core: 2. Of those that a mesh axis runs over, the one named last changes fastest.
Arguments:
- tokens: bfloat16 [4, 24576, 1024], P('dp', 'ctx'), may hold values from -6 to 6
- modality: int32 [4, 24576], P('dp', 'ctx'), may hold values 0 or 1
- type_embed: bfloat16 [2, 1024], replicated, may hold values from -6 to 6
- dest_shard: int32 [4, 24576], P('dp'), may hold values from 0 to 63, as said below
- dest_row: int32 [4, 24576], P('dp'), may hold values from 0 to 383, as said below
- segments: int32 [4, 24576], P('dp'), may hold values from 0 to 127, never falling along the last dimension, each value on 1 to 384 neighbouring positions
- w_qkv: bfloat16 [1024, 3072], P('ctx', 'dp')
- w_out: bfloat16 [1024, 1024], P('ctx', 'dp'), may hold values from -0.1875 to 0.1875
- w_up: bfloat16 [1024, 2048], P('ctx', 'dp'), may hold values from -0.1875 to 0.1875
- w_down: bfloat16 [2048, 1024], P('ctx', 'dp'), may hold values from -0.125 to 0.125
Outputs:
- encoded: bfloat16 [4, 24576, 1024], P('dp', 'ctx')
Inputs may be any that keep to these rules, and one draw needn't show every extreme that they name: For each sequence, dest_shard and dest_row together map its 24576 tokens one to one onto the 24576 packed positions. Among the tokens of one device (aligned blocks of 384), at most 12 have the same dest_shard, and in every draw some block has exactly 12 for some shard. `dest_row`: see dest_shard. `segments`: segment numbers never fall along a sequence; each segment holds 1 to 384 positions.
All inputs are finite; a program needn't handle non-finite values. No bound on the sum of `modality` on one device may be relied on, other than what follows from the above.
Results may differ from a plain program's by a relative error of at most 0.006.
Values may be sent and summed in bfloat16 or wider, within the bound.
A program may use at most 128 MiB of HBM per device.

v0:
```python
import jax
import jax.numpy as jnp
from jax import lax
from jax.sharding import Mesh
from jax.sharding import PartitionSpec as P

HEADS = 16
CTX = ("ctx_0", "ctx_1", "ctx_2")


norm_eps = 1e-06


def split_up(value, dim, devices):
    before, after = (value.shape[:dim], value.shape[dim + 1 :])
    return jnp.moveaxis(value.reshape(*before, devices, -1, *after), dim, 0)


def laid_out(blocks, dim):
    dims = list(blocks.shape[1:])
    dims[dim] *= blocks.shape[0]
    return jnp.moveaxis(blocks, 0, dim).reshape(dims)


def moved_by_axis(blocks, axes, turns):
    dims = [lax.axis_size(a) for a in axes]
    blocks = blocks.reshape(*dims, *blocks.shape[1:])
    for k in turns:
        blocks = lax.all_to_all(blocks, axes[k], split_axis=k, concat_axis=k, tiled=True)
    return blocks.reshape(-1, *blocks.shape[len(axes) :])


def two_step_exchange(value, groups, turns, split_dim, concat_dim):
    devices = lax.axis_size(groups[0]) * lax.axis_size(groups[1])
    blocks = split_up(value, split_dim, devices)
    return laid_out(moved_by_axis(blocks, groups, turns), concat_dim)


def gather_packed(arrays, axis, dims):
    vector = jnp.concatenate([a.reshape(-1) for a in arrays])
    lines, at, gathered = (lax.all_gather(vector, axis), 0, [])
    for a, dim in zip(arrays, dims):
        blocks = lines[:, at : at + a.size].reshape(-1, *a.shape)
        gathered.append(laid_out(blocks, dim))
        at += a.size
    return tuple(gathered)


def extended(value, sides, width):
    for axis, dim in sides:
        devices, length = (lax.axis_size(axis), value.shape[dim])
        up = [(i, (i + 1) % devices) for i in range(devices - 1)]
        down = [(j, i) for i, j in up]
        last = lax.slice_in_dim(value, length - width, length, axis=dim)
        initial = lax.slice_in_dim(value, 0, width, axis=dim)
        before = lax.ppermute(last, axis, up)
        after = lax.ppermute(initial, axis, down)
        value = jnp.concatenate([before, value, after], axis=dim)
    return value


def in_one_piece(arrays, axis, dim, along):
    ends, at = ([], 0)
    for a in arrays[:-1]:
        at += a.shape[along]
        ends.append(at)
    both = jnp.concatenate(arrays, axis=along)
    return tuple(jnp.split(lax.all_gather(both, axis, axis=dim, tiled=True), ends, axis=along))


def layer_norm(values):
    row_mean = jnp.mean(values, axis=-1, keepdims=True)
    centered = values - row_mean
    spread = jnp.mean(centered * centered, axis=-1, keepdims=True)
    return centered * lax.rsqrt(spread + norm_eps)


def attend(queries, key_pairs, query_seg, key_seg, head_count):
    seq_rows, model_width = queries.shape
    key_span = key_pairs.shape[0]
    groups = head_count // 4
    head_dim = model_width // head_count
    query_groups = queries.reshape(seq_rows, groups, 4, head_dim).transpose(1, 0, 2, 3)
    key_groups = (
        key_pairs[:, :model_width].reshape(key_span, groups, 4, head_dim).transpose(1, 0, 2, 3)
    )
    value_groups = (
        key_pairs[:, model_width:].reshape(key_span, groups, 4, head_dim).transpose(1, 0, 2, 3)
    )
    allowed = query_seg[:, None] == key_seg[None, :]
    score_scale = head_dim ** (-0.5)

    def one_group(operands):
        query_part, key_part, value_part = operands
        scores = (
            jnp.einsum("qhd,khd->hqk", query_part, key_part, preferred_element_type=jnp.float32)
            * score_scale
        )
        scores = jnp.where(allowed[None], scores, -1e30)
        row_max = jnp.max(scores, axis=-1, keepdims=True)
        expd = jnp.exp(scores - row_max)
        attn_probs = (expd / jnp.sum(expd, axis=-1, keepdims=True)).astype(jnp.bfloat16)
        return jnp.einsum(
            "hqk,khd->qhd", attn_probs, value_part, preferred_element_type=jnp.float32
        )

    head_mix = lax.map(one_group, (query_groups, key_groups, value_groups))
    return head_mix.transpose(1, 0, 2, 3).reshape(seq_rows, model_width).astype(jnp.bfloat16)


def local(tokens, modality, type_embed, dest_shard, dest_row, segments, w_qkv, w_out, w_up, w_down):
    shards = lax.axis_size(CTX)
    own_index = lax.axis_index(CTX)
    seq_rows = tokens.shape[1]
    model_width = tokens.shape[2]
    capacity = 2 * seq_rows // shards
    slot_total = shards * capacity
    extra = jnp.where(modality[0][:, None] == 1, type_embed[1], type_embed[0]).astype(jnp.float32)
    embedded = (tokens[0].astype(jnp.float32) + extra).astype(jnp.bfloat16)
    plan_shard = dest_shard[0].reshape(shards, seq_rows)
    plan_row = dest_row[0].reshape(shards, seq_rows)
    owners = jnp.arange(shards, dtype=jnp.int32)
    row_ids = jnp.arange(seq_rows, dtype=jnp.int32)
    slot_ids = jnp.arange(slot_total, dtype=jnp.int32)
    before = (row_ids[:, None] > row_ids[None, :]).astype(jnp.bfloat16)
    own_plan = lax.dynamic_index_in_dim(plan_shard, own_index, 0, keepdims=False)
    chosen = own_plan[:, None] == owners[None, :]
    earlier_all = jnp.dot(before, chosen.astype(jnp.bfloat16), preferred_element_type=jnp.float32)
    earlier = jnp.sum(jnp.where(chosen, earlier_all, 0.0), axis=1).astype(jnp.int32)
    outgoing_slot = own_plan * capacity + earlier
    slot_hit = outgoing_slot[None, :] == slot_ids[:, None]
    slot_token = jnp.sum(jnp.where(slot_hit, row_ids[None, :], 0), axis=1)
    slot_full = jnp.any(slot_hit, axis=1)
    outbox_rows = jnp.where(slot_full[:, None], embedded[slot_token], jnp.zeros((), jnp.bfloat16))
    inbox_rows = two_step_exchange(
        outbox_rows.reshape(shards, capacity, model_width),
        (("ctx_0", "ctx_1"), "ctx_2"),
        (1, 0),
        0,
        0,
    )
    arriving = plan_shard == own_index
    arrival_order = jnp.dot(
        arriving.astype(jnp.bfloat16), before.T, preferred_element_type=jnp.float32
    ).astype(jnp.int32)
    slot_numbers = jnp.arange(capacity, dtype=jnp.int32)
    slot_match = arriving[:, None, :] & (arrival_order[:, None, :] == slot_numbers[None, :, None])
    slot_row = jnp.sum(jnp.where(slot_match, plan_row[:, None, :], 0), axis=2).reshape(-1)
    slot_live = jnp.any(slot_match, axis=2).reshape(-1)
    place_hit = slot_live[:, None] & (slot_row[:, None] == row_ids[None, :])
    lookup = jnp.sum(jnp.where(place_hit, slot_ids[:, None], 0), axis=0)
    packed = inbox_rows.reshape(slot_total, model_width)[lookup]
    normed = layer_norm(packed.astype(jnp.float32)).astype(jnp.bfloat16)
    qkv_cols, out_cols, up_cols, down_cols = gather_packed(
        (w_qkv, w_out, w_up, w_down), "dp", (1, 1, 1, 1)
    )
    key_source = extended(normed, ((CTX, 0),), seq_rows)
    full_qkv, full_out, full_up, full_down = (
        *in_one_piece((qkv_cols, out_cols, up_cols), CTX, 0, 1),
        lax.all_gather(down_cols, CTX, axis=0, tiled=True),
    )
    queries = jnp.dot(normed, full_qkv[:, :model_width], preferred_element_type=jnp.float32)
    key_pairs = jnp.dot(key_source, full_qkv[:, model_width:], preferred_element_type=jnp.float32)
    queries = queries.astype(jnp.bfloat16)
    key_pairs = key_pairs.astype(jnp.bfloat16)
    seq_seg = segments[0]
    filler = jnp.full((seq_rows,), -1, jnp.int32)
    padded_seg = jnp.concatenate([filler, seq_seg, filler])
    key_seg = lax.dynamic_slice_in_dim(padded_seg, own_index * seq_rows, 3 * seq_rows, 0)
    query_seg = lax.dynamic_slice_in_dim(seq_seg, own_index * seq_rows, seq_rows, 0)
    attended = attend(queries, key_pairs, query_seg, key_seg, HEADS)
    projected = jnp.dot(attended, full_out, preferred_element_type=jnp.float32)
    middle = packed.astype(jnp.float32) + projected
    normed_mid = layer_norm(middle).astype(jnp.bfloat16)
    raised = jnp.dot(normed_mid, full_up, preferred_element_type=jnp.float32)
    hidden = jax.nn.gelu(raised, approximate=True).astype(jnp.bfloat16)
    lowered = jnp.dot(hidden, full_down, preferred_element_type=jnp.float32)
    result = (middle + lowered).astype(jnp.bfloat16)
    back_rows = jnp.where(slot_live[:, None], result[slot_row], jnp.zeros((), jnp.bfloat16))
    returned = lax.all_to_all(
        back_rows.reshape(shards, capacity, model_width),
        CTX,
        split_axis=0,
        concat_axis=0,
        tiled=True,
    )
    return returned.reshape(slot_total, model_width)[outgoing_slot][None]


def solution(mesh):
    torus = Mesh(mesh.devices.reshape(mesh.shape["dp"], 4, 8, 2), ("dp", "ctx_0", "ctx_1", "ctx_2"))
    return jax.shard_map(
        local,
        mesh=torus,
        in_specs=(
            P("dp", CTX, None),
            P("dp", CTX),
            P(),
            P("dp", None),
            P("dp", None),
            P("dp", None),
            P(CTX, "dp"),
            P(CTX, "dp"),
            P(CTX, "dp"),
            P(CTX, "dp"),
        ),
        out_specs=P("dp", CTX, None),
        check_vma=False,
    )
```

profile of v0, /device:TPU:1, one launch (start us, length us, event | category | flops | bytes accessed | tf_op | source)
XLA Modules:
  0.0 296.1 jit_solution(13546356378523316195)
XLA Ops:
  9.6 11.2 %all-gather = bf16[131072]{0:T(1024)(128)(2,1)S(1)} all-gather(bf16[32768]{0:T(1024)(128)(2,1)S(1)} %pad_maximum_fusion.1), channel_id=2, replica_groups=mesh['dp'=4,'ctx_0'=4,'ctx_1'=8,'ctx_2'=2] {'dp'}, dimensions={0}, use_global_device_ids=true | all-gather | bytes 327680 | tf_op jit(solution)/shard_map/all_gather | solution.py:41
  24.2 3.6 %gather_fusion = bf16[768,1024]{1,0:T(8,128)(2,1)} fusion(bf16[384,1024]{1,0:T(8,128)(2,1)S(1)} %fusion.78, s32[1024]{0:T(1024)S(1)} %pad_clamp_fusion.3), kind=kCustom, calls=%fused_computation | custom fusion | bytes 3148800 | tf_op jit(solution)/shard_map/gather | solution.py:134
  31.5 9.1 %all_to_all.15 = bf16[32,2,1,12,1024]{4,0,3,2,1:T(8,128)(2,1)S(1)} all-to-all(bf16[32,2,1,12,1024]{4,0,3,2,1:T(8,128)(2,1)S(1)} %copy.24), channel_id=1, replica_groups=mesh['dp'=4,'ctx_0'=4,'ctx_1'=8,'ctx_2'=2] {'ctx_2'}, dimensions={1} | all-to-all | bytes 3145728 | tf_op jit(solution)/shard_map/all_to_all | solution.py:29
  43.5 9.7 %all-to-all-start.1 = ((bf16[32,2,1,12,1024]{4,1,3,2,0:T(2,128)(2,1)}), bf16[32,2,1,12,1024]{4,1,3,2,0:T(2,128)(2,1)S(1)}, u32[]{:S(2)}, u32[]{:S(2)}) async-start(bf16[32,2,1,12,1024]{4,1,3,2,0:T(2,128)(2,1)} %copy.25), calls=%async_computation.1 | async-start | bytes 3145728 | tf_op jit(solution)/shard_map/all_to_all | solution.py:29
  55.9 38.5 %all-to-all-done.1 = bf16[32,2,1,12,1024]{4,1,3,2,0:T(2,128)(2,1)S(1)} async-done(((bf16[32,2,1,12,1024]{4,1,3,2,0:T(2,128)(2,1)}), bf16[32,2,1,12,1024]{4,1,3,2,0:T(2,128)(2,1)S(1)}, u32[]{:S(2)}, u32[]{:S(2)}) %all-to-all-start.1) | async-done | bytes 1572896 | tf_op jit(solution)/shard_map/all_to_all | solution.py:29
  101.7 9.8 %collective-permute-start = (bf16[384,1024]{1,0:T(8,128)(2,1)S(1)}, bf16[384,1024]{1,0:T(8,128)(2,1)S(1)}, u32[]{:S(2)}, u32[]{:S(2)}) collective-permute-start(bf16[384,1024]{1,0:T(8,128)(2,1)S(1)} %fusion.77), channel_id=1, source_target_pairs={{0,1},{1,2},{2,3},{3,4},{4,5},{5,6},{6,7},{7,8},{8,9},{9,10},{10,1... | collective-permute-start | bytes 2359304 | tf_op jit(solution)/shard_map/ppermute | solution.py:56
  114.6 14.5 %collective-permute-done = bf16[384,1024]{1,0:T(8,128)(2,1)S(1)} collective-permute-done((bf16[384,1024]{1,0:T(8,128)(2,1)S(1)}, bf16[384,1024]{1,0:T(8,128)(2,1)S(1)}, u32[]{:S(2)}, u32[]{:S(2)}) %collective-permute-start) | collective-permute-done | bytes 786464 | tf_op jit(solution)/shard_map/ppermute | solution.py:56
  131.4 8.7 %convolution_convert_fusion = bf16[1152,2048]{1,0:T(8,128)(2,1)S(1)} fusion(bf16[1024,6144]{1,0:T(8,128)(2,1)} %all-gather.4.cloned.1.call-done, bf16[384,1024]{1,0:T(8,128)(2,1)} %collective-permute-done.1, bf16[384,1024]{1,0:T(8,128)(2,1)S(1)} %fusion.77, bf16[384,1024]{1,0:T(8,128)(2,1)S(1)} %collective-permute-done), kind=kOutput, calls=%fused_computation.39 | convolution fusion | flops 4841275392 | bytes 11272192 | tf_op jit(solution)/shard_map/dot_general | solution.py:163
  142.0 4.3 %copy.31 = bf16[1152,1024]{0,1:T(8,128)(2,1)} copy(bf16[1152,1024]{1,0:T(8,128)(2,1)} %get-tuple-element.72) | data formatting | bytes 4718592 | tf_op jit(solution)/shard_map/slice | solution.py:85
  148.8 3.8 %fusion.81 = bf16[384,1024]{1,0:T(8,128)(2,1)} fusion(bf16[384,1024]{1,0:T(8,128)(2,1)} %copy-done.2, bf16[1024,6144]{1,0:T(8,128)(2,1)} %all-gather.4.cloned.1.call-done), kind=kOutput, calls=%fused_computation.75 | convolution fusion | flops 805699584 | bytes 3670016 | tf_op jit(solution)/shard_map/dot_general | solution.py:162
  154.1 32.4 %while.11 = (s32[]{:T(128)}, bf16[4,384,4,64]{1,3,2,0:T(8,128)(2,1)S(1)}, bf16[4,1152,4,64]{1,3,2,0:T(8,128)(2,1)}, bf16[4,384,4,64]{1,3,2,0:T(8,128)(2,1)S(1)},...) while((s32[]{:T(128)}, ...), condition=%wide.region_11.12_spmd.clone, body=%wide.region_8.11_spmd.clone.sunk | while | flops 695848704 | bytes 3904597 | solution.py:107
  154.5 3.6 %fusion.132 = f32[4,384]{1,0:T(4,128)S(1)} fusion(pred[384,1152]{1,0:T(8,128)(4,1)S(1)} %broadcast_compare_fusion.3, bf16[4,1152,4,64]{1,3,2,0:T(8,128)(2,1)} %get-tuple-element.141, s32[]{:T(128)} %get-tuple-element.129, bf16[4,384,4,64]{1,3,2,0:T(8,128)(2,1)S(1)} %get-tuple-element.140), kind=kOutput, calls=%fused_computation.131.clone.1 | convolution fusion | flops 233571456 | bytes 1235968 | tf_op jit(solution)/shard_map/while/body/eval_jaxpr/sub | solution.py:101
  158.1 4.1 %fusion.133 = bf16[4,384,4,64]{1,3,2,0:T(8,128)(2,1)S(1)} fusion(bf16[4,384,4,64]{1,3,2,0:T(8,128)(2,1)S(1)} %get-tuple-element.130, s32[]{:T(128)} %get-tuple-element.129, f32[4,384]{1,0:T(4,128)S(1)} %fusion.132, bf16[4,1152,4,64]{1,3,2,0:T(8,128)(2,1)} %get-tuple-element.139, pred[384,1152]{1,0:T(8,128)(4,1)S(1)} %broadcast_compare_fusion.3, ...), kind=kOutput, calls=%fused_computation.16.clone.1 | convolution fusion | flops 461834880 | bytes 2220032 | tf_op jit(solution)/shard_map/while/body/eval_jaxpr/hqk,khd->qhd/dot_general | solution.py:103
  162.5 3.6 %fusion.132 = f32[4,384]{1,0:T(4,128)S(1)} fusion(pred[384,1152]{1,0:T(8,128)(4,1)S(1)} %broadcast_compare_fusion.3, bf16[4,1152,4,64]{1,3,2,0:T(8,128)(2,1)} %get-tuple-element.141, s32[]{:T(128)} %get-tuple-element.129, bf16[4,384,4,64]{1,3,2,0:T(8,128)(2,1)S(1)} %get-tuple-element.140), kind=kOutput, calls=%fused_computation.131.clone.1 | convolution fusion | flops 233571456 | bytes 1235968 | tf_op jit(solution)/shard_map/while/body/eval_jaxpr/sub | solution.py:101
  166.2 4.1 %fusion.133 = bf16[4,384,4,64]{1,3,2,0:T(8,128)(2,1)S(1)} fusion(bf16[4,384,4,64]{1,3,2,0:T(8,128)(2,1)S(1)} %get-tuple-element.130, s32[]{:T(128)} %get-tuple-element.129, f32[4,384]{1,0:T(4,128)S(1)} %fusion.132, bf16[4,1152,4,64]{1,3,2,0:T(8,128)(2,1)} %get-tuple-element.139, pred[384,1152]{1,0:T(8,128)(4,1)S(1)} %broadcast_compare_fusion.3, ...), kind=kOutput, calls=%fused_computation.16.clone.1 | convolution fusion | flops 461834880 | bytes 2220032 | tf_op jit(solution)/shard_map/while/body/eval_jaxpr/hqk,khd->qhd/dot_general | solution.py:103
  170.6 3.6 %fusion.132 = f32[4,384]{1,0:T(4,128)S(1)} fusion(pred[384,1152]{1,0:T(8,128)(4,1)S(1)} %broadcast_compare_fusion.3, bf16[4,1152,4,64]{1,3,2,0:T(8,128)(2,1)} %get-tuple-element.141, s32[]{:T(128)} %get-tuple-element.129, bf16[4,384,4,64]{1,3,2,0:T(8,128)(2,1)S(1)} %get-tuple-element.140), kind=kOutput, calls=%fused_computation.131.clone.1 | convolution fusion | flops 233571456 | bytes 1235968 | tf_op jit(solution)/shard_map/while/body/eval_jaxpr/sub | solution.py:101
  174.2 4.1 %fusion.133 = bf16[4,384,4,64]{1,3,2,0:T(8,128)(2,1)S(1)} fusion(bf16[4,384,4,64]{1,3,2,0:T(8,128)(2,1)S(1)} %get-tuple-element.130, s32[]{:T(128)} %get-tuple-element.129, f32[4,384]{1,0:T(4,128)S(1)} %fusion.132, bf16[4,1152,4,64]{1,3,2,0:T(8,128)(2,1)} %get-tuple-element.139, pred[384,1152]{1,0:T(8,128)(4,1)S(1)} %broadcast_compare_fusion.3, ...), kind=kOutput, calls=%fused_computation.16.clone.1 | convolution fusion | flops 461834880 | bytes 2220032 | tf_op jit(solution)/shard_map/while/body/eval_jaxpr/hqk,khd->qhd/dot_general | solution.py:103
  178.6 3.6 %fusion.132 = f32[4,384]{1,0:T(4,128)S(1)} fusion(pred[384,1152]{1,0:T(8,128)(4,1)S(1)} %broadcast_compare_fusion.3, bf16[4,1152,4,64]{1,3,2,0:T(8,128)(2,1)} %get-tuple-element.141, s32[]{:T(128)} %get-tuple-element.129, bf16[4,384,4,64]{1,3,2,0:T(8,128)(2,1)S(1)} %get-tuple-element.140), kind=kOutput, calls=%fused_computation.131.clone.1 | convolution fusion | flops 233571456 | bytes 1235968 | tf_op jit(solution)/shard_map/while/body/eval_jaxpr/sub | solution.py:101
  182.3 4.1 %fusion.133 = bf16[4,384,4,64]{1,3,2,0:T(8,128)(2,1)S(1)} fusion(bf16[4,384,4,64]{1,3,2,0:T(8,128)(2,1)S(1)} %get-tuple-element.130, s32[]{:T(128)} %get-tuple-element.129, f32[4,384]{1,0:T(4,128)S(1)} %fusion.132, bf16[4,1152,4,64]{1,3,2,0:T(8,128)(2,1)} %get-tuple-element.139, pred[384,1152]{1,0:T(8,128)(4,1)S(1)} %broadcast_compare_fusion.3, ...), kind=kOutput, calls=%fused_computation.16.clone.1 | convolution fusion | flops 461834880 | bytes 2220032 | tf_op jit(solution)/shard_map/while/body/eval_jaxpr/hqk,khd->qhd/dot_general | solution.py:103
  189.6 22.3 %all-gather.6.cloned.1.call-done = bf16[2048,1024]{1,0:T(8,128)(2,1)} async-done(((bf16[32,1024]{1,0:T(8,128)(2,1)}), bf16[2048,1024]{1,0:T(8,128)(2,1)}) %all-gather.6.cloned.1.call-update) | async-done | bytes 4194320 | tf_op jit(solution)/shard_map/all_gather | solution.py:160
  212.0 7.1 %add_convert_fusion = bf16[384,1024]{1,0:T(8,128)(2,1)S(1)} fusion(f32[384,1024]{1,0:T(8,128)S(1)} %get-tuple-element.77, bf16[2048,1024]{1,0:T(8,128)(2,1)} %all-gather.6.cloned.1.call-done, bf16[1024,6144]{1,0:T(8,128)(2,1)} %all-gather.4.cloned.1.call-done, f32[384]{0:T(512)S(1)} %add_rsqrt_fusion, f32[384]{0:T(512)S(1)} %broadcast_multiply_fusion), kind=kOutput, calls=%fused_computation.72 | convolution fusion | flops 3230269440 | bytes 12324864 | tf_op jit(solution)/shard_map/dot_general | solution.py:177
  219.1 3.6 %gather_fusion.2 = bf16[768,1024]{1,0:T(8,128)(2,1)} fusion(bf16[384,1024]{1,0:T(8,128)(2,1)S(1)} %add_convert_fusion, s32[1024]{0:T(1024)S(1)} %pad_clamp_fusion.1), kind=kCustom, calls=%fused_computation.2 | custom fusion | bytes 3148800 | tf_op jit(solution)/shard_map/gather | solution.py:179
  226.6 6.3 %all-to-all-start.2 = ((bf16[64,12,1024]{2,1,0:T(8,128)(2,1)}), bf16[64,12,1024]{2,1,0:T(8,128)(2,1)}, u32[]{:S(2)}, u32[]{:S(2)}) async-start(bf16[64,12,1024]{2,1,0:T(8,128)(2,1)} %broadcast_select_fusion.1), calls=%async_computation.2 | async-start | bytes 4194304 | tf_op jit(solution)/shard_map/all_to_all | solution.py:180
  233.0 51.1 %all-to-all-done.2 = bf16[64,12,1024]{2,1,0:T(8,128)(2,1)} async-done(((bf16[64,12,1024]{2,1,0:T(8,128)(2,1)}), bf16[64,12,1024]{2,1,0:T(8,128)(2,1)}, u32[]{:S(2)}, u32[]{:S(2)}) %all-to-all-start.2) | async-done | bytes 1572896 | tf_op jit(solution)/shard_map/all_to_all | solution.py:180
  (101 shorter events, 47.4 us)
Async XLA Ops:
  6.5 15.8 %copy-start.4 = (s32[1,24576]{1,0:T(1,128)S(1)}, s32[1,24576]{1,0:T(1,128)}, u32[]{:S(2)}) copy-start(s32[1,24576]{1,0:T(1,128)} %param.15) | copy-start | bytes 294916
  6.5 17.3 %copy-start.7 = (s32[1,384]{1,0:T(1,128)S(1)}, s32[1,384]{1,0:T(1,128)}, u32[]{:S(2)}) copy-start(s32[1,384]{1,0:T(1,128)} %param.13) | copy-start | bytes 4612
  6.5 17.3 %copy-start.6 = (bf16[2,1024]{1,0:T(2,128)(2,1)S(1)}, bf16[2,1024]{1,0:T(2,128)(2,1)}, u32[]{:S(2)}) copy-start(bf16[2,1024]{1,0:T(2,128)(2,1)} %param.14) | copy-start | bytes 12292
  6.5 17.4 %copy-start.1 = (bf16[1,384,1024]{2,1,0:T(8,128)(2,1)S(1)}, bf16[1,384,1024]{2,1,0:T(8,128)(2,1)}, u32[]{:S(2)}) copy-start(bf16[1,384,1024]{2,1,0:T(8,128)(2,1)} %param.12) | copy-start | bytes 2359300
  6.5 124.8 %all-gather.4.cloned.1.call-start = ((), (), s32[]{:S(2)}) async-start(), calls=%async_computation.3 | async-start | bytes 12779520 | tf_op jit(solution)/shard_map/all_gather | solution.py:68
  43.5 9.7 %copy-start.5 = (s32[1,24576]{1,0:T(1,128)S(1)}, s32[1,24576]{1,0:T(1,128)}, u32[]{:S(2)}) copy-start(s32[1,24576]{1,0:T(1,128)} %param.16) | copy-start | bytes 294916
  43.5 50.8 %all-to-all-start.1 = ((bf16[32,2,1,12,1024]{4,1,3,2,0:T(2,128)(2,1)}), bf16[32,2,1,12,1024]{4,1,3,2,0:T(2,128)(2,1)S(1)}, u32[]{:S(2)}, u32[]{:S(2)}) async-start(bf16[32,2,1,12,1024]{4,1,3,2,0:T(2,128)(2,1)} %copy.25), calls=%async_computation.1 | async-start | bytes 3145728 | tf_op jit(solution)/shard_map/all_to_all | solution.py:29
  53.2 158.8 %all-gather.6.cloned.1.call-start = ((), (), s32[]{:S(2)}) async-start(), calls=%async_computation.4 | async-start | bytes 4259840 | tf_op jit(solution)/shard_map/all_gather | solution.py:160
  100.9 13.6 %copy-start.3 = (s32[1,24576]{1,0:T(1,128)S(1)}, s32[1,24576]{1,0:T(1,128)}, u32[]{:S(2)}) copy-start(s32[1,24576]{1,0:T(1,128)} %param.17) | copy-start | bytes 294916
  101.7 29.7 %copy-start.2 = (bf16[384,1024]{1,0:T(8,128)(2,1)}, bf16[384,1024]{1,0:T(8,128)(2,1)S(1)}, u32[]{:S(2)}) copy-start(bf16[384,1024]{1,0:T(8,128)(2,1)S(1)} %fusion.77) | copy-start | bytes 2359300
  101.7 27.4 %collective-permute-start = (bf16[384,1024]{1,0:T(8,128)(2,1)S(1)}, bf16[384,1024]{1,0:T(8,128)(2,1)S(1)}, u32[]{:S(2)}, u32[]{:S(2)}) collective-permute-start(bf16[384,1024]{1,0:T(8,128)(2,1)S(1)} %fusion.77), channel_id=1, source_target_pairs={{0,1},{1,2},{2,3},{3,4},{4,5},{5,6},{6,7},{7,8},{8,9},{9,10},{10,1... | collective-permute-start | bytes 2359304 | tf_op jit(solution)/shard_map/ppermute | solution.py:56
  111.6 18.8 %collective-permute-start.1 = (bf16[384,1024]{1,0:T(8,128)(2,1)S(1)}, bf16[384,1024]{1,0:T(8,128)(2,1)}, u32[]{:S(2)}, u32[]{:S(2)}) collective-permute-start(bf16[384,1024]{1,0:T(8,128)(2,1)S(1)} %fusion.77), channel_id=1, source_target_pairs={{1,0},{2,1},{3,2},{4,3},{5,4},{6,5},{7,6},{8,7},{9,8},{10,9},{11,1... | collective-permute-start | bytes 2359304 | tf_op jit(solution)/shard_map/ppermute | solution.py:57
  148.8 5.3 %copy-start = (bf16[4,384,4,64]{1,3,2,0:T(8,128)(2,1)S(1)}, bf16[4,384,4,64]{1,3,2,0:T(8,128)(2,1)}, u32[]{:S(2)}) copy-start(bf16[4,384,4,64]{1,3,2,0:T(8,128)(2,1)} %custom-call.8) | copy-start | bytes 2359300
  226.6 57.5 %all-to-all-start.2 = ((bf16[64,12,1024]{2,1,0:T(8,128)(2,1)}), bf16[64,12,1024]{2,1,0:T(8,128)(2,1)}, u32[]{:S(2)}, u32[]{:S(2)}) async-start(bf16[64,12,1024]{2,1,0:T(8,128)(2,1)} %broadcast_select_fusion.1), calls=%async_computation.2 | async-start | bytes 4194304 | tf_op jit(solution)/shard_map/all_to_all | solution.py:180
Sparse Core Ops, SparseCore 0:
  22.0 109.3 all-gather.3
  134.1 77.7 all-gather.5
where the time goes:
time: 297 us; the launch traced here: 296 us
  waiting for transfers between devices  129 us (43%)
  matrix products  53.6 us (18%)
  local copies, waits for them, and re-layouts  42.7 us (14%)
  starting transfers between devices  28 us (9%)
  blocking collectives  20.4 us (7%)
  between operations  13.8 us (5%)
  other arithmetic  8.47 us (3%)
    all_to_all x1, waiting for transfers between devices, local(): lax.all_to_all(back_rows.reshape(shards, capacity, model_width), CTX, spl...  51.1 us
    all_to_all x1, waiting for transfers between devices, moved_by_axis(): lax.all_to_all(blocks, axes[k], split_axis=k, concat_axis=k, tiled=True)  38.5 us
    all_gather x1, waiting for transfers between devices, local(): lax.all_gather(down_cols, CTX, axis=0, tiled=True)  22.3 us
    dot_general x4, matrix products, one_group(): jnp.einsum('hqk,khd->qhd', attn_probs, value_part, preferred_element_type...  16.3 us
    sub x4, matrix products, one_group(): expd = jnp.exp(scores - row_max)  14.6 us
    ppermute x1, waiting for transfers between devices, extended(): before = lax.ppermute(last, axis, up)  14.5 us
    all_gather x1, blocking collectives, gather_packed(): lines, at, gathered = (lax.all_gather(vector, axis), 0, [])  11.2 us
    ppermute x1, starting transfers between devices, extended(): before = lax.ppermute(last, axis, up)  9.83 us
  transfers between devices with their start and end apart: 6, of which 6 were waited for; matrix products, arithmetic and copies ran while one was open for 27% of the time, Pallas kernels for 0%

commit v1 on v0

v1 whole, which is shorter than its diff:
```python
import jax
import jax.numpy as jnp
from jax import lax
from jax.experimental import pallas as pl
from jax.experimental.pallas import tpu as pltpu
from jax.sharding import Mesh
from jax.sharding import PartitionSpec as P

MESH = pl.DeviceIdType.MESH
CTX = ("ctx_0", "ctx_1", "ctx_2")
AXES = ("dp", *CTX)
NX, NZ, NY = 4, 8, 4
CHIPS = NX * NZ
ROWS = 384
WIDTH = 1024
HEADS = 16
FF = 2048
CAP = 12
BLOCK = 2 * CAP
SLOTS = CHIPS * BLOCK
BAND = 896
bf16, f32, i32 = jnp.bfloat16, jnp.float32, jnp.int32


def layer_norm(values):
    row_mean = jnp.mean(values, axis=-1, keepdims=True)
    centered = values - row_mean
    spread = jnp.mean(centered * centered, axis=-1, keepdims=True)
    return centered * lax.rsqrt(spread + 1e-06)


def dot(a, b):
    return jnp.dot(a, b, preferred_element_type=f32)


def iota(shape, dim):
    return lax.broadcasted_iota(i32, shape, dim)


def turned(row):
    return jnp.transpose(jnp.broadcast_to(row, (128, row.shape[1])))


def lanes(start, size):
    return pl.ds(pl.multiple_of(start, 128), size)


def kernel(
    tok, mod, temb, dsh, drow, seg, w_qkv, w_out, w_up, w_down, out,
    g_qkv, g_out, g_up, g_down, plan_s, plan_r, outbox, inbox, back, home,
    pick_back, pick_home, bias, packed, normed, q, k, v, att, mid, nmid, hidden, res,
    a_send, a_recv, ad_send, ad_recv, r_send, r_recv, rd_send, rd_recv, local_sem,
    z_send, z_recv, x_send, x_recv, y_send, y_recv, f_send, f_recv, d_send, d_recv,
    h_send, h_recv,
):
    y, x, z, c = [lax.axis_index(a) for a in AXES]
    chip = x * NZ + z
    own = 2 * chip + c
    partner = (y, x, z, 1 - c)
    shards = (w_qkv, w_out, w_up, w_down)
    full = (g_qkv, g_out, g_up, g_down)

    def place(j):
        tx = lax.rem(x + j // NZ, NX)
        tz = lax.rem(z + lax.rem(j, NZ), NZ)
        return tx, tz

    def remote(src, dst, send, recv, device):
        return pltpu.make_async_remote_copy(
            src_ref=src, dst_ref=dst, send_sem=send, recv_sem=recv,
            device_id=device, device_id_type=MESH,
        )

    right_chip = lax.rem(chip + 1, CHIPS)
    left_chip = lax.rem(chip + CHIPS - 1, CHIPS)
    far_chip = c * right_chip + (1 - c) * left_chip
    far = (y, far_chip // NZ, lax.rem(far_chip, NZ), 1 - c)

    barrier = pltpu.get_barrier_semaphore()

    def greet(j, _):
        tx, tz = place(j)
        pl.semaphore_signal(barrier, inc=1, device_id=(y, tx, tz, c), device_id_type=MESH)
        return 0

    lax.fori_loop(1, CHIPS, greet, 0)
    pl.semaphore_signal(barrier, inc=1, device_id=partner, device_id_type=MESH)
    pl.semaphore_signal(barrier, inc=1, device_id=far, device_id_type=MESH)
    for step in (1, NY - 1):
        pl.semaphore_signal(
            barrier, inc=1, device_id=(lax.rem(y + step, NY), x, z, c), device_id_type=MESH
        )

    def mine(w, col):
        size = shards[w].shape[1]
        return lanes(col * size, size)

    own_copies = [
        pltpu.make_async_copy(shards[w], full[w].at[chip, c, :, mine(w, y)], local_sem.at[w])
        for w in range(4)
    ]
    for cp in own_copies:
        cp.start()

    own_plan = dsh[:, lanes(own * ROWS, ROWS)]
    owner_ids = iota((64, ROWS), 0)
    chosen = owner_ids == own_plan
    before = (iota((ROWS, ROWS), 0) < iota((ROWS, ROWS), 1)).astype(bf16)
    ranks = dot(chosen.astype(f32).astype(bf16), before)
    earlier = jnp.sum(jnp.where(chosen, ranks, 0.0), axis=0, keepdims=True).astype(i32)
    slot = own_plan * CAP + earlier
    kinds = turned(mod[...])[:, :1]
    types = temb[...].astype(f32)
    extra = jnp.where(kinds == 1, types[1:2], types[0:1])
    att[...] = (tok[...].astype(f32) + extra).astype(bf16)

    pl.semaphore_wait(barrier, CHIPS - 1 + 4)

    def z_copy(w, j):
        return remote(
            shards[w], full[w].at[chip, c, :, mine(w, y)], z_send.at[w, j], z_recv.at[w, j],
            (y, x, lax.rem(z + j, NZ), c),
        )

    def x_copy(w, j):
        part = full[w].at[pl.ds(x * NZ, NZ), c, :, mine(w, y)]
        return remote(
            part, part, x_send.at[w, j], x_recv.at[w, j], (y, lax.rem(x + j, NX), z, c)
        )

    def y_copy(w, side):
        part = full[w].at[:, c, :, mine(w, y)]
        to = lax.rem(y + (1, NY - 1)[side], NY)
        return remote(part, part, y_send.at[w, side], y_recv.at[w, side], (to, x, z, c))

    def f_copy(w, side):
        held = lax.rem(y + (NY - 1, 1)[side], NY)
        part = full[w].at[pl.ds(side * (CHIPS // 2), CHIPS // 2), c, :, mine(w, held)]
        to = lax.rem(y + (1, NY - 1)[side], NY)
        return remote(part, part, f_send.at[w, side], f_recv.at[w, side], (to, x, z, c))

    def d_copy(w, step):
        part = full[w].at[:, c, :, mine(w, lax.rem(y + step, NY))]
        return remote(part, part, d_send.at[w, step], d_recv.at[w, step], partner)

    def each(count, act):
        def step(j, _):
            act(j)
            return 0

        lax.fori_loop(1, count, step, 0)

    def z_start(ws):
        for w in ws:
            each(NZ, lambda j: z_copy(w, j).start())

    def x_start(ws):
        for w in ws:
            own_copies[w].wait()
            each(NZ, lambda j: z_copy(w, j).wait())
            each(NX, lambda j: x_copy(w, j).start())

    def y_start(ws):
        for w in ws:
            each(NX, lambda j: x_copy(w, j).wait())
            y_copy(w, 0).start()
            y_copy(w, 1).start()
            d_copy(w, 0).start()

    def f_start(ws):
        for w in ws:
            y_copy(w, 0).wait()
            y_copy(w, 1).wait()
            f_copy(w, 0).start()
            f_copy(w, 1).start()
            d_copy(w, 1).start()
            d_copy(w, 3).start()

    def last_start(ws):
        for w in ws:
            f_copy(w, 0).wait()
            f_copy(w, 1).wait()
            d_copy(w, 2).start()

    def weights_done(w):
        for step in range(NY):
            d_copy(w, step).wait()

    first, rest = (0,), (1, 2, 3)
    z_start(first)

    embedded = att[...]

    def order(j):
        return (j // NZ) * NZ + lax.rem(3 * j, NZ)

    def a_copy(j):
        tx, tz = place(j)
        return remote(
            outbox.at[tx * NZ + tz], inbox.at[0, chip], a_send.at[j], a_recv.at[j], (y, tx, tz, c)
        )

    def pack(j, _):
        pick = (iota((SLOTS // NX, ROWS), 0) + j * (SLOTS // NX) == slot).astype(f32).astype(bf16)
        rows = dot(pick, embedded).astype(bf16)
        for i in range(NZ):
            outbox[j * NZ + i] = rows[i * BLOCK : (i + 1) * BLOCK]
        return 0

    lax.fori_loop(0, NX, pack, 0)
    own_block = pltpu.make_async_copy(outbox.at[chip], inbox.at[0, chip], local_sem.at[4])
    own_block.start()

    WAVE = 4

    def send_wave(n):
        def step(i, _):
            a_copy(order(i)).start()
            return 0

        lax.fori_loop(max(n * WAVE, 1), (n + 1) * WAVE, step, 0)

    def drain_wave(n):
        def step(i, _):
            a_copy(order(i)).wait_send()
            return 0

        lax.fori_loop(max(n * WAVE, 1), (n + 1) * WAVE, step, 0)

    send_wave(0)
    send_wave(1)
    x_start(first)

    def spread(j, _):
        part = lanes(j * ROWS, ROWS)
        plan_s[pl.ds(j, 1), :] = dsh[:, part]
        plan_r[pl.ds(j, 1), :] = drow[:, part]
        return 0

    drain_wave(0)
    send_wave(2)
    lax.fori_loop(0, 64, spread, 0)
    arriving = plan_s[...] == own
    arrival = dot(arriving.astype(f32).astype(bf16), before)
    rows_plus = plan_r[...].astype(f32) + 1.0
    drain_wave(1)
    send_wave(3)
    y_start(first)
    z_start(rest)
    slot_ids = iota((64, 128), 1)
    table = jnp.zeros((64, 128), f32)
    for n in range(CAP):
        hit = jnp.logical_and(arriving, arrival == float(n))
        value = jnp.sum(jnp.where(hit, rows_plus, 0.0), axis=1, keepdims=True)
        table = jnp.where(slot_ids == n, value, table)
    high = jnp.floor(table * (1.0 / 16.0))
    low = table - 16.0 * high
    lane = iota((128, SLOTS), 1)
    expand = (iota((128, SLOTS), 0) == lax.rem(lane, CAP)).astype(f32).astype(bf16)
    wide = 16.0 * dot(high.astype(bf16), expand) + dot(low.astype(bf16), expand)
    lane = iota((64, SLOTS), 1)
    source = iota((64, SLOTS), 0)

    def looked_up(wanted):
        return jnp.sum(jnp.where(source == wanted, wide, 0.0), axis=0, keepdims=True).astype(i32) - 1

    back_rows = looked_up(lane // CAP)
    other_rows = looked_up(2 * (lane // BLOCK) + (1 - c))
    lane_row = iota((1, SLOTS), 1)
    to_me = lax.rem(lane_row // CAP, 2) == c
    here_rows = jnp.where(to_me, back_rows, -1)
    other_rows = jnp.where(to_me, other_rows, -1)
    drain_wave(2)
    send_wave(4)
    f_start(first)
    x_start(rest)
    back_cols = turned(back_rows)
    for n in range(ROWS // 128):
        pick_back[:, 128 * n : 128 * (n + 1)] = (
            (back_cols == iota((SLOTS, 128), 1) + 128 * n).astype(f32).astype(bf16)
        )
    home_lane = (lax.rem(own_plan, 2) + c) % 2
    home_slot = home_lane * SLOTS + (own_plan // 2) * BLOCK + c * CAP + earlier
    home_cols = turned(home_slot)
    for n in range(2 * SLOTS // 128):
        pick_home[:, 128 * n : 128 * (n + 1)] = (
            (home_cols == iota((ROWS, 128), 1) + 128 * n).astype(f32).astype(bf16)
        )
    drain_wave(3)
    send_wave(5)

    q_seg = seg[:, lanes(own * ROWS, ROWS)]
    left_seg = seg[:, lanes(jnp.maximum(own - 1, 0) * ROWS, ROWS)]
    right_seg = seg[:, lanes(jnp.minimum(own + 1, 63) * ROWS, ROWS)]
    left_seg = jnp.where(own == 0, -1, left_seg)
    right_seg = jnp.where(own == 63, -1, right_seg)
    k_seg = jnp.concatenate([left_seg, q_seg, right_seg], axis=1)
    q_cols = turned(q_seg)
    for a in range(3):
        for n in range(BAND // 128):
            keys = k_seg[:, 128 * (a + n) : 128 * (a + n + 1)]
            same = q_cols[128 * a : 128 * (a + 1)] == keys
            bias[a, :, 128 * n : 128 * (n + 1)] = jnp.where(same, 0.0, -1e30)

    drain_wave(4)
    send_wave(6)
    last_start(first)
    drain_wave(5)
    send_wave(7)
    y_start(rest)
    drain_wave(6)
    drain_wave(7)

    def forward(src, send, recv, n):
        part = lax.rem(x + NX - n, NX)
        return remote(
            src.at[0, pl.ds(part * NZ, NZ)], src.at[1, pl.ds(part * NZ, NZ)],
            send.at[n], recv.at[n], partner,
        )

    own_block.wait()
    for n in range(NX):

        def arrive(j, _):
            a_copy(j).wait_recv()
            return 0

        lax.fori_loop(max(n * NZ, 1), (n + 1) * NZ, arrive, 0)
        forward(inbox, ad_send, ad_recv, n).start()
    for n in range(NX):
        forward(inbox, ad_send, ad_recv, n).wait()

    pick_here = (iota((ROWS, SLOTS), 0) == here_rows).astype(f32).astype(bf16)
    pick_other = (iota((ROWS, SLOTS), 0) == other_rows).astype(f32).astype(bf16)
    rows = dot(pick_here, inbox[0].reshape(SLOTS, WIDTH)) + dot(
        pick_other, inbox[1].reshape(SLOTS, WIDTH)
    )
    packed[...] = rows.astype(bf16)
    normed[1] = layer_norm(rows).astype(bf16)

    def h_copy(side):
        goes_right = c == 1 if side else c == 0
        slot = jnp.where(goes_right, 0, 2)
        return remote(
            normed.at[1], normed.at[slot], h_send.at[side], h_recv.at[side], (partner, far)[side]
        )

    h_copy(0).start()
    h_copy(1).start()

    weights_done(0)
    TILE = 256

    def columns(rows, weight, start, count, store):
        def step(j, _):
            part = lanes(start + j * TILE, TILE)
            w = weight[:, :, :, part]
            store(j, dot(rows, w.reshape(w.shape[0] * w.shape[1] * w.shape[2], TILE)))
            return 0

        lax.fori_loop(0, count // TILE, step, 0)

    def store_q(j, value):
        q[:, lanes(j * TILE, TILE)] = (value * 0.125).astype(bf16)

    def store_kv(block):
        at = pl.ds(block * ROWS, ROWS)

        def store_k(j, value):
            k[at, lanes(j * TILE, TILE)] = value.astype(bf16)

        def store_v(j, value):
            v[at, lanes(j * TILE, TILE)] = value.astype(bf16)

        return store_k, store_v

    own_rows = normed[1]
    columns(own_rows, g_qkv, 0, WIDTH, store_q)
    for block, side in ((1, None), (None, 0), (None, 1)):
        if side is not None:
            h_copy(side).wait()
        else:
            store_k, store_v = store_kv(1)
            columns(own_rows, g_qkv, WIDTH, WIDTH, store_k)
            columns(own_rows, g_qkv, 2 * WIDTH, WIDTH, store_v)
    for block in (0, 2):
        near_rows = normed[block]
        store_k, store_v = store_kv(block)
        columns(near_rows, g_qkv, WIDTH, WIDTH, store_k)
        columns(near_rows, g_qkv, 2 * WIDTH, WIDTH, store_v)
    f_start(rest)

    low_half = iota((128, 128), 1) < 64

    def attend(a):
        def step(h, _):
            part = lanes(h * 128, 128)
            rows = slice(128 * a, 128 * (a + 1))
            span = slice(128 * a, 128 * a + BAND)
            queries, keys, values = q[rows, part], k[span, part], v[span, part]
            mixed = []
            for half in (low_half, jnp.logical_not(low_half)):
                picked = jnp.where(half, queries.astype(f32), 0.0).astype(bf16)
                scores = lax.dot_general(
                    picked, keys, (((1,), (1,)), ((), ())), preferred_element_type=f32
                )
                scores = scores + bias[a]
                expd = jnp.exp(scores - jnp.max(scores, axis=1, keepdims=True))
                total = jnp.sum(expd, axis=1, keepdims=True)
                mixed.append(dot(expd.astype(bf16), values) / total)
            att[rows, part] = jnp.where(low_half, mixed[0], mixed[1]).astype(bf16)
            return 0

        lax.fori_loop(0, HEADS // 2, step, 0)

    attend(0)
    attend(1)
    last_start(rest)
    attend(2)

    weights_done(1)

    def store_mid(j, value):
        part = lanes(j * TILE, TILE)
        mid[:, part] = packed[:, part].astype(f32) + value

    columns(att[...], g_out, 0, WIDTH, store_mid)
    nmid[...] = layer_norm(mid[...]).astype(bf16)
    weights_done(2)

    def store_hidden(j, value):
        hidden[:, lanes(j * TILE, TILE)] = jax.nn.gelu(value, approximate=True).astype(bf16)

    columns(nmid[...], g_up, 0, FF, store_hidden)
    weights_done(3)

    def store_res(j, value):
        part = lanes(j * TILE, TILE)
        res[:, part] = (mid[:, part] + value).astype(bf16)

    columns(hidden[...], g_down, 0, WIDTH, store_res)

    result = res[...]

    def r_copy(j):
        tx, tz = place(j)
        return remote(
            back.at[tx * NZ + tz], home.at[0, chip], r_send.at[j], r_recv.at[j], (y, tx, tz, c)
        )

    def pack_back(j, _):
        at = pl.ds(pl.multiple_of(j * (SLOTS // NX), 16), SLOTS // NX)
        rows = dot(pick_back[at, :], result).astype(bf16)
        for i in range(NZ):
            back[j * NZ + i] = rows[i * BLOCK : (i + 1) * BLOCK]
        return 0

    lax.fori_loop(0, NX, pack_back, 0)
    home_block = pltpu.make_async_copy(back.at[chip], home.at[0, chip], local_sem.at[5])
    home_block.start()
    each(CHIPS, lambda i: r_copy(order(i)).start())
    home_block.wait()
    for n in range(NX):

        def arrive_home(j, _):
            r_copy(j).wait_recv()
            return 0

        lax.fori_loop(max(n * NZ, 1), (n + 1) * NZ, arrive_home, 0)
        forward(home, rd_send, rd_recv, n).start()
    for n in range(NX):
        forward(home, rd_send, rd_recv, n).wait()
    out[...] = (
        dot(pick_home[:, :SLOTS], home[0].reshape(SLOTS, WIDTH))
        + dot(pick_home[:, SLOTS:], home[1].reshape(SLOTS, WIDTH))
    ).astype(bf16)
    each(CHIPS, lambda i: r_copy(i).wait_send())


def local(tokens, modality, type_embed, dest_shard, dest_row, segments, w_qkv, w_out, w_up, w_down):
    vmem = pl.BlockSpec(memory_space=pltpu.VMEM)
    dma = pltpu.SemaphoreType.DMA
    V = pltpu.VMEM
    result = pl.pallas_call(
        kernel,
        out_shape=jax.ShapeDtypeStruct((ROWS, WIDTH), bf16),
        in_specs=[vmem] * 10,
        out_specs=vmem,
        scratch_shapes=[
            V((CHIPS, 2, 16, 3 * WIDTH), bf16),
            V((CHIPS, 2, 16, WIDTH), bf16),
            V((CHIPS, 2, 16, FF), bf16),
            V((CHIPS, 2, 32, WIDTH), bf16),
            V((64, ROWS), i32),
            V((64, ROWS), i32),
            V((CHIPS, BLOCK, WIDTH), bf16),
            V((2, CHIPS, BLOCK, WIDTH), bf16),
            V((CHIPS, BLOCK, WIDTH), bf16),
            V((2, CHIPS, BLOCK, WIDTH), bf16),
            V((SLOTS, ROWS), bf16),
            V((ROWS, 2 * SLOTS), bf16),
            V((3, 128, BAND), f32),
            V((ROWS, WIDTH), bf16),
            V((3, ROWS, WIDTH), bf16),
            V((ROWS, WIDTH), bf16),
            V((3 * ROWS, WIDTH), bf16),
            V((3 * ROWS, WIDTH), bf16),
            V((ROWS, WIDTH), bf16),
            V((ROWS, WIDTH), f32),
            V((ROWS, WIDTH), bf16),
            V((ROWS, FF), bf16),
            V((ROWS, WIDTH), bf16),
            dma((CHIPS,)), dma((CHIPS,)), dma((NX,)), dma((NX,)),
            dma((CHIPS,)), dma((CHIPS,)), dma((NX,)), dma((NX,)), dma((6,)),
            dma((4, NZ)), dma((4, NZ)), dma((4, NX)), dma((4, NX)),
            dma((4, 2)), dma((4, 2)), dma((4, 2)), dma((4, 2)), dma((4, NY)), dma((4, NY)),
            dma((2,)), dma((2,)),
        ],
        compiler_params=pltpu.CompilerParams(
            collective_id=0, has_side_effects=True, vmem_limit_bytes=63 * 1024 * 1024
        ),
        name="encoder",
    )(tokens[0], modality, type_embed, dest_shard, dest_row, segments, w_qkv, w_out, w_up, w_down)
    return result[None]


def solution(mesh):
    torus = Mesh(mesh.devices.reshape(NY, NX, NZ, 2), AXES)
    return jax.shard_map(
        local,
        mesh=torus,
        in_specs=(
            P("dp", CTX, None),
            P("dp", CTX),
            P(),
            P("dp", None),
            P("dp", None),
            P("dp", None),
            P(CTX, "dp"),
            P(CTX, "dp"),
            P(CTX, "dp"),
            P(CTX, "dp"),
        ),
        out_specs=P("dp", CTX, None),
        check_vma=False,
    )
```

time: 297 us -> 173 us (0.58)
  Pallas kernels: 0 us -> 171 us
  waiting for transfers between devices: 129 us -> 0 us
  matrix products: 53.6 us -> 0 us
  local copies, waits for them, and re-layouts: 42.7 us -> 2.06 us
  starting transfers between devices: 28 us -> 0 us
  blocking collectives: 20.4 us -> 0 us
  between operations: 13.8 us -> 0.01 us
  other arithmetic: 8.47 us -> 0 us
    pallas_call x0 -> x1, Pallas kernels: none -> 171 us  [local(): pl.pallas_call(kernel, out_shape=jax.ShapeDtypeStruct((ROWS, WIDTH), bf16...]
    all_to_all x2 -> x0, waiting for transfers between devices: 89.5 us -> none  [the longest x1 51.1 us: local(): lax.all_to_all(back_rows.reshape(shards, capacity, model_width), CTX, spl...]
    dot_general x10 -> x0, matrix products: 39 us -> none  [the longest x4 16.3 us: one_group(): jnp.einsum('hqk,khd->qhd', attn_probs, value_part, preferred_element_type...]
    all_gather x2 -> x0, waiting for transfers between devices: 23.3 us -> none  [the longest x1 22.3 us: local(): lax.all_gather(down_cols, CTX, axis=0, tiled=True)]
    gather x6 -> x0, local copies, waits for them, and re-layouts: 16.6 us -> none  [the longest x2 5.94 us: local(): embedded[slot_token]]
    all_to_all x2 -> x0, starting transfers between devices: 16 us -> none  [the longest x1 9.69 us: moved_by_axis(): lax.all_to_all(blocks, axes[k], split_axis=k, concat_axis=k, tiled=True)]
    ppermute x2 -> x0, waiting for transfers between devices: 15.8 us -> none  [the longest x1 14.5 us: extended(): before = lax.ppermute(last, axis, up)]
    sub x4 -> x0, matrix products: 14.6 us -> none  [one_group(): expd = jnp.exp(scores - row_max)]
  transfers between devices with their start and end apart: 6 -> 0, of which waited for: 6 -> 0; matrix products, arithmetic and copies ran while one was open for 27% -> 0% of each run, Pallas kernels for 0% -> 0%
where the time goes in v1:
time: 173 us
  Pallas kernels  171 us (99%)
  local copies, waits for them, and re-layouts  2.06 us (1%)
    pallas_call x1, Pallas kernels, local(): pl.pallas_call(kernel, out_shape=jax.ShapeDtypeStruct((ROWS, WIDTH), bf16...  171 us

profile of v1, /device:TPU:1, one launch (start us, length us, event | category | flops | bytes accessed | tf_op | source)
XLA Modules:
  0.0 172.6 jit_solution(15577764519512805309)
XLA Ops:
  0.0 170.6 %encoder.1 = bf16[384,1024]{1,0:T(8,128)(2,1)} custom-call(bf16[384,1024]{1,0:T(8,128)(2,1)} %bitcast.3, s32[1,384]{1,0:T(1,128)} %mod.1, bf16[2,1024]{1,0:T(2,128)(2,1)} %temb.1, s32[1,24576]{1,0:T(1,128)} %dsh.1, s32[1,24576]{1,0:T(1,128)} %drow.1, s32[1,24576]{1,0:T(1,128)} %seg.1, bf16[16,768]{1,0:T(8,128)(2,1)} %w_qkv.1, bf16[16,256]{1,0:T(8,128)(2,1)} %w_out.1, ...), custom_call_target="tpu_custom_call" | custom-call | tf_op jit(solution)/shard_map/encoder/pallas_call | solution.py:484
  170.6 2.1 %copy.12 = bf16[1,384,1024]{2,1,0:T(8,128)(2,1)} copy(bf16[1,384,1024]{2,1,0:T(8,128)(2,1)} %bitcast.2) | data formatting | bytes 1572864

commit v2 on v1

v2 whole, which is shorter than its diff:
```python
import jax
import jax.numpy as jnp
from jax import lax
from jax.experimental import pallas as pl
from jax.experimental.pallas import tpu as pltpu
from jax.sharding import Mesh
from jax.sharding import PartitionSpec as P

MESH = pl.DeviceIdType.MESH
CTX = ("ctx_0", "ctx_1", "ctx_2")
AXES = ("dp", *CTX)
NX, NZ, NY = 4, 8, 4
CHIPS = NX * NZ
ROWS = 384
WIDTH = 1024
HEADS = 16
FF = 2048
CAP = 12
BLOCK = 2 * CAP
SLOTS = CHIPS * BLOCK
BAND = 896
bf16, f32, i32 = jnp.bfloat16, jnp.float32, jnp.int32


def layer_norm(values):
    row_mean = jnp.mean(values, axis=-1, keepdims=True)
    centered = values - row_mean
    spread = jnp.mean(centered * centered, axis=-1, keepdims=True)
    return centered * lax.rsqrt(spread + 1e-06)


def dot(a, b):
    return jnp.dot(a, b, preferred_element_type=f32)


def iota(shape, dim):
    return lax.broadcasted_iota(i32, shape, dim)


def turned(row):
    return jnp.transpose(jnp.broadcast_to(row, (128, row.shape[1])))


def lanes(start, size):
    return pl.ds(pl.multiple_of(start, 128), size)


def kernel(
    tok, mod, temb, dsh, drow, seg, w_qkv, w_out, w_up, w_down, out,
    g_qkv, g_out, g_up, g_down, plan_s, plan_r, outbox, inbox, back, home,
    pick_back, pick_home, bias, packed, normed, q, k, v, att, mid, nmid, hidden, res,
    a_send, a_recv, ad_send, ad_recv, r_send, r_recv, rd_send, rd_recv,
    z_send, z_recv, q_recv, x_send, x_recv, y_send, y_recv, f_send, f_recv, d_send, d_recv,
    h_send, h_recv,
):
    y, x, z, c = [lax.axis_index(a) for a in AXES]
    chip = x * NZ + z
    own = 2 * chip + c
    partner = (y, x, z, 1 - c)
    shards = (w_qkv, w_out, w_up, w_down)
    full = (g_qkv, g_out, g_up, g_down)

    def place(j):
        tx = lax.rem(x + j // NZ, NX)
        tz = lax.rem(z + lax.rem(j, NZ), NZ)
        return tx, tz

    def remote(src, dst, send, recv, device):
        return pltpu.make_async_remote_copy(
            src_ref=src, dst_ref=dst, send_sem=send, recv_sem=recv,
            device_id=device, device_id_type=MESH,
        )

    def await_bytes(ref, sem):
        pltpu.make_async_copy(ref, ref, sem).wait()

    right_chip = lax.rem(chip + 1, CHIPS)
    left_chip = lax.rem(chip + CHIPS - 1, CHIPS)
    far_chip = c * right_chip + (1 - c) * left_chip
    far = (y, far_chip // NZ, lax.rem(far_chip, NZ), 1 - c)

    barrier = pltpu.get_barrier_semaphore()

    def greet(j, _):
        tx, tz = place(j)
        pl.semaphore_signal(barrier, inc=1, device_id=(y, tx, tz, c), device_id_type=MESH)
        return 0

    lax.fori_loop(1, CHIPS, greet, 0)
    pl.semaphore_signal(barrier, inc=1, device_id=partner, device_id_type=MESH)
    pl.semaphore_signal(barrier, inc=1, device_id=far, device_id_type=MESH)
    for step in range(1, NY):
        pl.semaphore_signal(
            barrier, inc=1, device_id=(lax.rem(y + step, NY), x, z, c), device_id_type=MESH
        )

    def mine(w, col):
        size = shards[w].shape[1]
        return lanes(col * size, size)

    own_copies = [
        pltpu.make_async_copy(shards[w], full[w].at[chip, c, :, mine(w, y)], z_recv.at[w])
        for w in range(4)
    ]
    for cp in own_copies:
        cp.start()

    own_plan = dsh[:, lanes(own * ROWS, ROWS)]
    owner_ids = iota((64, ROWS), 0)
    chosen = owner_ids == own_plan
    before = (iota((ROWS, ROWS), 0) < iota((ROWS, ROWS), 1)).astype(bf16)
    ranks = dot(chosen.astype(f32).astype(bf16), before)
    earlier = jnp.sum(jnp.where(chosen, ranks, 0.0), axis=0, keepdims=True).astype(i32)
    slot = own_plan * CAP + earlier
    kinds = turned(mod[...])[:, :1]
    types = temb[...].astype(f32)
    extra = jnp.where(kinds == 1, types[1:2], types[0:1])
    att[...] = (tok[...].astype(f32) + extra).astype(bf16)

    embedded = att[...]

    def pack(j, _):
        pick = (iota((SLOTS // NX, ROWS), 0) + j * (SLOTS // NX) == slot).astype(f32).astype(bf16)
        rows = dot(pick, embedded).astype(bf16)
        for i in range(NZ):
            outbox[j * NZ + i] = rows[i * BLOCK : (i + 1) * BLOCK]
        return 0

    lax.fori_loop(0, NX, pack, 0)

    pl.semaphore_wait(barrier, CHIPS - 1 + 5)

    def at_y(w):
        return w != 3

    def block(w, middle, last):
        xi, yi = (middle, last) if at_y(w) else (last, middle)
        return full[w].at[pl.ds(xi * NZ, NZ), c, :, mine(w, yi)]

    def spot(w):
        return (x, y) if at_y(w) else (y, x)

    def device(w, middle, last):
        return (last, middle, z, c) if at_y(w) else (middle, last, z, c)

    def around(i, step):
        return lax.rem(i + 4 + step, 4)

    def z_copy(w, j):
        return remote(
            shards[w], full[w].at[chip, c, :, mine(w, y)], z_send.at[w], z_recv.at[w],
            (y, x, lax.rem(z + j, NZ), c),
        )

    def ring_copy(w, step, side):
        way = (1, NZ - 1)[side]
        held = lax.rem(z + (step - 1) * (NZ - way), NZ)
        part = full[w].at[x * NZ + held, c, :, mine(w, y)]
        src = shards[w] if step == 1 else part
        to = (y, x, lax.rem(z + way, NZ), c)
        return remote(src, part, z_send.at[w], q_recv.at[w - 1, step - 1, side], to)

    def ring_sides(w, step):
        return (0, 1) if step < 4 else (0,) if w < 3 else (1,)

    def ring_wait(step):
        for w in rest:
            for side in ring_sides(w, step):
                ring_copy(w, step, side).wait_recv()

    def ring_start(step):
        if step > 1:
            ring_wait(step - 1)
        for w in rest:
            for side in ring_sides(w, step):
                ring_copy(w, step, side).start()

    def m_copy(w, j):
        m, n = spot(w)
        part = block(w, m, n)
        return remote(part, part, x_send.at[w], x_recv.at[w, j], device(w, lax.rem(m + j, 4), n))

    def n_copy(w, side):
        m, n = spot(w)
        step = (1, -1)[side]
        xi, yi = (around(m, -step), n) if at_y(w) else (n, around(m, -step))
        half = NZ // 2
        ref = full[w].at[pl.ds(xi * NZ + side * half, half), c, :, mine(w, yi)]
        to = device(w, around(m, step), n)
        return remote(ref, ref, x_send.at[w], x_recv.at[w, 2 * side], to)

    def l_copy(w, side, part):
        m, n = spot(w)
        ref = block(w, around(m, -part), n)
        to = device(w, m, around(n, (1, -1)[side]))
        return remote(ref, ref, y_send.at[w], y_recv.at[w, side, part], to)

    def f_copy(w, part):
        m, n = spot(w)
        step = 1 if part < 2 else -1
        ref = block(w, around(m, -part), around(n, -step))
        to = device(w, m, around(n, step))
        return remote(ref, ref, f_send.at[w], f_recv.at[w], to)

    def d_copy(w, step):
        at = around(spot(w)[1], step)
        if at_y(w):
            part = full[w].at[:, c, :, mine(w, at)]
        else:
            part = full[w].at[pl.ds(at * NZ, NZ), c]
        return remote(part, part, d_send.at[w], d_recv.at[w], partner)

    def each(count, act):
        def step(j, _):
            act(j)
            return 0

        lax.fori_loop(1, count, step, 0)

    def z_start(w):
        each(NZ, lambda j: z_copy(w, j).start())

    def l_part(w, part):
        l_copy(w, 0, part).start()
        l_copy(w, 1, part).start()

    def m_start(w):
        if w == 0:
            await_bytes(full[w].at[pl.ds(x * NZ, NZ), c, :, mine(w, y)], z_recv.at[w])
        else:
            own_copies[w].wait()
        await_bytes(full[w].at[pl.ds(0, NZ - 1), c, :, mine(w, y)], z_send.at[w])
        m_copy(w, 1).start()
        m_copy(w, 3).start()
        l_part(w, 0)

    def l_start(w):
        m_copy(w, 1).wait_recv()
        n_copy(w, 0).start()
        l_part(w, 1)
        m_copy(w, 3).wait_recv()
        n_copy(w, 1).start()
        l_part(w, 3)

    def l_finish(w):
        n_copy(w, 0).wait_recv()
        n_copy(w, 1).wait_recv()
        l_part(w, 2)
        d_copy(w, 0).start()

    def f_start(w):
        for part in (0, 1, 3, 2):
            l_copy(w, 0, part).wait_recv()
            l_copy(w, 1, part).wait_recv()
            f_copy(w, part).start()
        d_copy(w, 1).start()
        d_copy(w, 3).start()

    def last_start(w):
        quarter = full[w].at[:, c, :, mine(w, 0)]
        await_bytes(quarter, f_recv.at[w])
        d_copy(w, 2).start()

    def weights_done(w):
        await_bytes(full[w].at[:, 1 - c], d_recv.at[w])

    def weights_sent(w):
        part = mine(w, 0)
        await_bytes(full[w].at[pl.ds(0, 3 * NZ), c, :, part], x_send.at[w])
        await_bytes(full[w].at[:, :, :, part], y_send.at[w])
        await_bytes(full[w].at[:, c, :, part], f_send.at[w])
        await_bytes(full[w].at[:, c], d_send.at[w])

    rest = (1, 2, 3)
    z_start(0)
    ring_start(1)

    def order(j):
        return (j // NZ) * NZ + lax.rem(3 * j, NZ)

    def place_wave(j):
        return 2 * (j // NZ) + lax.rem(3 * j, NZ) // WAVE

    WAVE = 4

    def a_copy(j):
        tx, tz = place(j)
        return remote(
            outbox.at[tx * NZ + tz], inbox.at[0, chip], a_send.at[place_wave(j)], a_recv.at[j // NZ], (y, tx, tz, c)
        )

    own_block = pltpu.make_async_copy(outbox.at[chip], inbox.at[0, chip], a_recv.at[0])
    own_block.start()

    def send_wave(n):
        def step(i, _):
            a_copy(order(i)).start()
            return 0

        lax.fori_loop(max(n * WAVE, 1), (n + 1) * WAVE, step, 0)

    def drain_wave(n):
        await_bytes(inbox.at[1, pl.ds(0, WAVE if n else WAVE - 1)], a_send.at[n])

    send_wave(0)
    send_wave(1)
    m_start(0)
    ring_start(2)

    def spread(j, _):
        part = lanes(j * ROWS, ROWS)
        plan_s[pl.ds(j, 1), :] = dsh[:, part]
        plan_r[pl.ds(j, 1), :] = drow[:, part]
        return 0

    drain_wave(0)
    send_wave(2)
    lax.fori_loop(0, 64, spread, 0)
    arriving = plan_s[...] == own
    arrival = dot(arriving.astype(f32).astype(bf16), before)
    rows_plus = plan_r[...].astype(f32) + 1.0
    drain_wave(1)
    send_wave(3)
    l_start(0)
    ring_start(3)
    slot_ids = iota((64, 128), 1)
    table = jnp.zeros((64, 128), f32)
    for n in range(CAP):
        hit = jnp.logical_and(arriving, arrival == float(n))
        value = jnp.sum(jnp.where(hit, rows_plus, 0.0), axis=1, keepdims=True)
        table = jnp.where(slot_ids == n, value, table)
    high = jnp.floor(table * (1.0 / 16.0))
    low = table - 16.0 * high
    lane = iota((128, SLOTS), 1)
    expand = (iota((128, SLOTS), 0) == lax.rem(lane, CAP)).astype(f32).astype(bf16)
    wide = 16.0 * dot(high.astype(bf16), expand) + dot(low.astype(bf16), expand)
    lane = iota((64, SLOTS), 1)
    source = iota((64, SLOTS), 0)

    def looked_up(wanted):
        return jnp.sum(jnp.where(source == wanted, wide, 0.0), axis=0, keepdims=True).astype(i32) - 1

    back_rows = looked_up(lane // CAP)
    other_rows = looked_up(2 * (lane // BLOCK) + (1 - c))
    lane_row = iota((1, SLOTS), 1)
    to_me = lax.rem(lane_row // CAP, 2) == c
    here_rows = jnp.where(to_me, back_rows, -1)
    other_rows = jnp.where(to_me, other_rows, -1)
    drain_wave(2)
    send_wave(4)
    l_finish(0)
    ring_start(4)
    back_cols = turned(back_rows)
    for n in range(ROWS // 128):
        pick_back[:, 128 * n : 128 * (n + 1)] = (
            (back_cols == iota((SLOTS, 128), 1) + 128 * n).astype(f32).astype(bf16)
        )
    home_lane = (lax.rem(own_plan, 2) + c) % 2
    home_slot = home_lane * SLOTS + (own_plan // 2) * BLOCK + c * CAP + earlier
    home_cols = turned(home_slot)
    for n in range(2 * SLOTS // 128):
        pick_home[:, 128 * n : 128 * (n + 1)] = (
            (home_cols == iota((ROWS, 128), 1) + 128 * n).astype(f32).astype(bf16)
        )
    drain_wave(3)
    send_wave(5)
    send_wave(6)
    send_wave(7)

    q_seg = seg[:, lanes(own * ROWS, ROWS)]
    left_seg = seg[:, lanes(jnp.maximum(own - 1, 0) * ROWS, ROWS)]
    right_seg = seg[:, lanes(jnp.minimum(own + 1, 63) * ROWS, ROWS)]
    left_seg = jnp.where(own == 0, -1, left_seg)
    right_seg = jnp.where(own == 63, -1, right_seg)
    k_seg = jnp.concatenate([left_seg, q_seg, right_seg], axis=1)
    q_cols = turned(q_seg)
    for a in range(3):
        for n in range(BAND // 128):
            keys = k_seg[:, 128 * (a + n) : 128 * (a + n + 1)]
            same = q_cols[128 * a : 128 * (a + 1)] == keys
            bias[a, :, 128 * n : 128 * (n + 1)] = jnp.where(same, 0.0, -1e30)

    f_start(0)
    ring_wait(4)
    for w in rest:
        m_start(w)
    drain_wave(4)
    drain_wave(5)
    drain_wave(6)
    drain_wave(7)
    last_start(0)

    def x_blocks(n):
        return pl.ds(lax.rem(x + NX - n, NX) * NZ, NZ)

    for n in range(NX):
        span = x_blocks(n)
        await_bytes(inbox.at[0, span], a_recv.at[n])
        remote(inbox.at[0, span], inbox.at[1, span], ad_send, ad_recv, partner).start()
    for w in rest:
        l_start(w)
    await_bytes(inbox.at[0], ad_send)
    await_bytes(inbox.at[1], ad_recv)

    pick_here = (iota((ROWS, SLOTS), 0) == here_rows).astype(f32).astype(bf16)
    pick_other = (iota((ROWS, SLOTS), 0) == other_rows).astype(f32).astype(bf16)
    rows = dot(pick_here, inbox[0].reshape(SLOTS, WIDTH)) + dot(
        pick_other, inbox[1].reshape(SLOTS, WIDTH)
    )
    packed[...] = rows.astype(bf16)
    normed[1] = layer_norm(rows).astype(bf16)

    NEAR = ROWS // 3
    pieces = ((0, NEAR), (NEAR, ROWS))

    def far_rows(n, begins):
        lo, hi = pieces[n]
        start = jnp.where(begins, lo, ROWS - hi)
        return pl.ds(pl.multiple_of(start, 128), hi - lo)

    near_copy = remote(
        normed.at[1], normed.at[2 * c], h_send.at[0], h_recv.at[0], partner
    )

    def far_copy(n):
        rows = far_rows(n, c == 0)
        return remote(
            normed.at[1, rows], normed.at[2 * (1 - c), rows], h_send.at[1 + n], h_recv.at[1 + n], far
        )

    near_copy.start()
    far_copy(0).start()
    far_copy(1).start()

    weights_done(0)
    TILE = 256

    def columns(rows, weight, start, count, store):
        def step(j, _):
            part = lanes(start + j * TILE, TILE)
            w = weight[:, :, :, part]
            store(j, dot(rows, w.reshape(w.shape[0] * w.shape[1] * w.shape[2], TILE)))
            return 0

        lax.fori_loop(0, count // TILE, step, 0)

    def store_q(j, value):
        q[:, lanes(j * TILE, TILE)] = (value * 0.125).astype(bf16)

    def keys_values(rows, at):
        def store_k(j, value):
            k[at, lanes(j * TILE, TILE)] = value.astype(bf16)

        def store_v(j, value):
            v[at, lanes(j * TILE, TILE)] = value.astype(bf16)

        columns(rows, g_qkv, WIDTH, WIDTH, store_k)
        columns(rows, g_qkv, 2 * WIDTH, WIDTH, store_v)

    def rows_at(start, size):
        return pl.ds(pl.multiple_of(start, 128), size)

    def far_keys(n):
        far_copy(n).wait()
        rows = far_rows(n, c == 1)
        keys_values(normed[2 * c, rows], rows_at(2 * c * ROWS + rows.start, rows.size))

    own_rows = normed[1]
    columns(own_rows, g_qkv, 0, WIDTH, store_q)
    keys_values(own_rows, rows_at(ROWS, ROWS))
    near_copy.wait()
    near = 2 * (1 - c)
    keys_values(normed[near], rows_at(near * ROWS, ROWS))
    for w in rest:
        l_finish(w)

    low_half = iota((128, 128), 1) < 64

    def attend(n):
        a = jnp.where(c == 1, n, 2 - n)
        rows = rows_at(128 * a, 128)
        span = rows_at(128 * a, BAND)

        def step(h, _):
            part = lanes(h * 128, 128)
            queries = q[rows, part].astype(f32)
            keys, values = k[span, part], v[span, part]
            both = jnp.concatenate(
                [jnp.where(low_half, queries, 0.0), jnp.where(low_half, 0.0, queries)], axis=0
            ).astype(bf16)
            scores = lax.dot_general(
                both, keys, (((1,), (1,)), ((), ())), preferred_element_type=f32
            )
            shut = bias[a]
            scores = jnp.concatenate([scores[:128] + shut, scores[128:] + shut], axis=0)
            expd = jnp.exp(scores - jnp.max(scores, axis=1, keepdims=True))
            total = jnp.sum(expd, axis=1, keepdims=True)
            mixed = dot(expd.astype(bf16), values) / total
            att[rows, part] = jnp.where(low_half, mixed[:128], mixed[128:]).astype(bf16)
            return 0

        lax.fori_loop(0, HEADS // 2, step, 0)

    far_keys(0)
    attend(0)
    for w in rest:
        f_start(w)
    far_keys(1)
    attend(1)
    last_start(1)
    attend(2)
    last_start(2)
    last_start(3)

    weights_done(1)

    def store_mid(j, value):
        part = lanes(j * TILE, TILE)
        mid[:, part] = packed[:, part].astype(f32) + value

    columns(att[...], g_out, 0, WIDTH, store_mid)
    nmid[...] = layer_norm(mid[...]).astype(bf16)
    weights_done(2)

    def store_hidden(j, value):
        hidden[:, lanes(j * TILE, TILE)] = jax.nn.gelu(value, approximate=True).astype(bf16)

    columns(nmid[...], g_up, 0, FF, store_hidden)
    weights_done(3)

    HALF = WIDTH // 2

    def r_copy(half, j):
        tx, tz = place(j)
        part = pl.ds(half * HALF, HALF)
        return remote(
            back.at[tx * NZ + tz, :, part], home.at[0, chip, :, part],
            r_send.at[half], r_recv.at[half, j // NZ], (y, tx, tz, c),
        )

    for half in range(2):
        part = slice(half * HALF, (half + 1) * HALF)

        def store_res(j, value):
            at = lanes(half * HALF + j * TILE, TILE)
            res[:, at] = (mid[:, at] + value).astype(bf16)

        columns(hidden[...], g_down, half * HALF, HALF, store_res)
        result = res[:, part]

        def pack_back(j, _):
            at = pl.ds(pl.multiple_of(j * (SLOTS // NX), 16), SLOTS // NX)
            rows = dot(pick_back[at, :], result).astype(bf16)
            for i in range(NZ):
                back[j * NZ + i, :, part] = rows[i * BLOCK : (i + 1) * BLOCK]
            return 0

        lax.fori_loop(0, NX, pack_back, 0)
        pltpu.make_async_copy(
            back.at[chip, :, pl.ds(half * HALF, HALF)],
            home.at[0, chip, :, pl.ds(half * HALF, HALF)],
            r_recv.at[half, 0],
        ).start()
        each(CHIPS, lambda i: r_copy(half, order(i)).start())

    for half in range(2):
        part = slice(half * HALF, (half + 1) * HALF)
        cols = pl.ds(half * HALF, HALF)
        for n in range(NX):
            span = x_blocks(n)
            await_bytes(home.at[0, span, :, cols], r_recv.at[half, n])
            remote(
                home.at[0, span, :, cols], home.at[1, span, :, cols],
                rd_send.at[half], rd_recv.at[half], partner,
            ).start()
        await_bytes(home.at[1, :, :, cols], rd_recv.at[half])
        out[:, part] = (
            dot(pick_home[:, :SLOTS], home[0, :, :, part].reshape(SLOTS, HALF))
            + dot(pick_home[:, SLOTS:], home[1, :, :, part].reshape(SLOTS, HALF))
        ).astype(bf16)
    for half in range(2):
        cols = pl.ds(half * HALF, HALF)
        await_bytes(home.at[0, pl.ds(0, CHIPS - 1), :, cols], r_send.at[half])
        await_bytes(home.at[0, :, :, cols], rd_send.at[half])
    for w in range(4):
        weights_sent(w)


def local(tokens, modality, type_embed, dest_shard, dest_row, segments, w_qkv, w_out, w_up, w_down):
    vmem = pl.BlockSpec(memory_space=pltpu.VMEM)
    dma = pltpu.SemaphoreType.DMA
    V = pltpu.VMEM
    result = pl.pallas_call(
        kernel,
        out_shape=jax.ShapeDtypeStruct((ROWS, WIDTH), bf16),
        in_specs=[vmem] * 10,
        out_specs=vmem,
        scratch_shapes=[
            V((CHIPS, 2, 16, 3 * WIDTH), bf16),
            V((CHIPS, 2, 16, WIDTH), bf16),
            V((CHIPS, 2, 16, FF), bf16),
            V((CHIPS, 2, 32, WIDTH), bf16),
            V((64, ROWS), i32),
            V((64, ROWS), i32),
            V((CHIPS, BLOCK, WIDTH), bf16),
            V((2, CHIPS, BLOCK, WIDTH), bf16),
            V((CHIPS, BLOCK, WIDTH), bf16),
            V((2, CHIPS, BLOCK, WIDTH), bf16),
            V((SLOTS, ROWS), bf16),
            V((ROWS, 2 * SLOTS), bf16),
            V((3, 128, BAND), f32),
            V((ROWS, WIDTH), bf16),
            V((3, ROWS, WIDTH), bf16),
            V((ROWS, WIDTH), bf16),
            V((3 * ROWS, WIDTH), bf16),
            V((3 * ROWS, WIDTH), bf16),
            V((ROWS, WIDTH), bf16),
            V((ROWS, WIDTH), f32),
            V((ROWS, WIDTH), bf16),
            V((ROWS, FF), bf16),
            V((ROWS, WIDTH), bf16),
            dma((8,)), dma((NX,)), dma, dma,
            dma((2,)), dma((2, NX)), dma((2,)), dma((2,)),
            dma((4,)), dma((4,)), dma((3, 4, 2)), dma((4,)), dma((4, 4)),
            dma((4,)), dma((4, 2, 4)), dma((4,)), dma((4,)), dma((4,)), dma((4,)),
            dma((3,)), dma((3,)),
        ],
        compiler_params=pltpu.CompilerParams(
            collective_id=0, has_side_effects=True, vmem_limit_bytes=63 * 1024 * 1024
        ),
        name="encoder",
    )(tokens[0], modality, type_embed, dest_shard, dest_row, segments, w_qkv, w_out, w_up, w_down)
    return result[None]


def solution(mesh):
    torus = Mesh(mesh.devices.reshape(NY, NX, NZ, 2), AXES)
    return jax.shard_map(
        local,
        mesh=torus,
        in_specs=(
            P("dp", CTX, None),
            P("dp", CTX),
            P(),
            P("dp", None),
            P("dp", None),
            P("dp", None),
            P(CTX, "dp"),
            P(CTX, "dp"),
            P(CTX, "dp"),
            P(CTX, "dp"),
        ),
        out_specs=P("dp", CTX, None),
        check_vma=False,
    )
```

time: 173 us -> 141 us (0.82)
  Pallas kernels: 171 us -> 139 us
    pallas_call x1, Pallas kernels: 171 us -> 139 us  [local(): pl.pallas_call(kernel, out_shape=jax.ShapeDtypeStruct((ROWS, WIDTH), bf16...]
where the time goes in v2:
time: 141 us
  Pallas kernels  139 us (99%)
  local copies, waits for them, and re-layouts  2.06 us (1%)
    pallas_call x1, Pallas kernels, local(): pl.pallas_call(kernel, out_shape=jax.ShapeDtypeStruct((ROWS, WIDTH), bf16...  139 us

profile of v2, /device:TPU:1, one launch (start us, length us, event | category | flops | bytes accessed | tf_op | source)
XLA Modules:
  0.0 141.3 jit_solution(12309820728368136012)
XLA Ops:
  0.0 139.2 %encoder.1 = bf16[384,1024]{1,0:T(8,128)(2,1)} custom-call(bf16[384,1024]{1,0:T(8,128)(2,1)} %bitcast.3, s32[1,384]{1,0:T(1,128)} %mod.1, bf16[2,1024]{1,0:T(2,128)(2,1)} %temb.1, s32[1,24576]{1,0:T(1,128)} %dsh.1, s32[1,24576]{1,0:T(1,128)} %drow.1, s32[1,24576]{1,0:T(1,128)} %seg.1, bf16[16,768]{1,0:T(8,128)(2,1)} %w_qkv.1, bf16[16,256]{1,0:T(8,128)(2,1)} %w_out.1, ...), custom_call_target="tpu_custom_call" | custom-call | tf_op jit(solution)/shard_map/encoder/pallas_call | solution.py:593
  139.2 2.1 %copy.12 = bf16[1,384,1024]{2,1,0:T(8,128)(2,1)} copy(bf16[1,384,1024]{2,1,0:T(8,128)(2,1)} %bitcast.2) | data formatting | bytes 1572864

commit v3 on v2

--- a/solution.py
+++ b/solution.py
@@ -46,7 +46,8 @@
 
 
 def kernel(
-    tok, mod, temb, dsh, drow, seg, w_qkv, w_out, w_up, w_down, out,
+    tok_in, mod_in, temb_in, dsh_in, drow_in, seg_in, w_qkv, w_out, w_up, w_down, out,
+    tok, mod, temb, dsh, drow, seg, in_sem, own_sem,
     g_qkv, g_out, g_up, g_down, plan_s, plan_r, outbox, inbox, back, home,
     pick_back, pick_home, bias, packed, normed, q, k, v, att, mid, nmid, hidden, res,
     a_send, a_recv, ad_send, ad_recv, r_send, r_recv, rd_send, rd_recv,
@@ -99,11 +100,19 @@
         return lanes(col * size, size)
 
     own_copies = [
-        pltpu.make_async_copy(shards[w], full[w].at[chip, c, :, mine(w, y)], z_recv.at[w])
+        pltpu.make_async_copy(shards[w], full[w].at[chip, c, :, mine(w, y)], own_sem.at[w])
         for w in range(4)
     ]
-    for cp in own_copies:
+    inputs = [
+        pltpu.make_async_copy(src, dst, in_sem.at[n])
+        for n, (src, dst) in enumerate(
+            ((dsh_in, dsh), (mod_in, mod), (temb_in, temb), (tok_in, tok), (drow_in, drow), (seg_in, seg))
+        )
+    ]
+    for cp in inputs[:4] + own_copies + inputs[4:]:
         cp.start()
+    for cp in inputs[:4]:
+        cp.wait()
 
     own_plan = dsh[:, lanes(own * ROWS, ROWS)]
     owner_ids = iota((64, ROWS), 0)
@@ -128,6 +137,8 @@
 
     lax.fori_loop(0, NX, pack, 0)
 
+    for cp in own_copies + inputs[4:]:
+        cp.wait()
     pl.semaphore_wait(barrier, CHIPS - 1 + 5)
 
     def at_y(w):
@@ -147,18 +158,15 @@
         return lax.rem(i + 4 + step, 4)
 
     def z_copy(w, j):
-        return remote(
-            shards[w], full[w].at[chip, c, :, mine(w, y)], z_send.at[w], z_recv.at[w],
-            (y, x, lax.rem(z + j, NZ), c),
-        )
+        part = full[w].at[chip, c, :, mine(w, y)]
+        return remote(part, part, z_send.at[w], z_recv.at[w], (y, x, lax.rem(z + j, NZ), c))
 
     def ring_copy(w, step, side):
         way = (1, NZ - 1)[side]
         held = lax.rem(z + (step - 1) * (NZ - way), NZ)
         part = full[w].at[x * NZ + held, c, :, mine(w, y)]
-        src = shards[w] if step == 1 else part
         to = (y, x, lax.rem(z + way, NZ), c)
-        return remote(src, part, z_send.at[w], q_recv.at[w - 1, step - 1, side], to)
+        return remote(part, part, z_send.at[w], q_recv.at[w - 1, step - 1, side], to)
 
     def ring_sides(w, step):
         return (0, 1) if step < 4 else (0,) if w < 3 else (1,)
@@ -224,35 +232,44 @@
         l_copy(w, 0, part).start()
         l_copy(w, 1, part).start()
 
-    def m_start(w):
-        if w == 0:
-            await_bytes(full[w].at[pl.ds(x * NZ, NZ), c, :, mine(w, y)], z_recv.at[w])
-        else:
-            own_copies[w].wait()
-        await_bytes(full[w].at[pl.ds(0, NZ - 1), c, :, mine(w, y)], z_send.at[w])
-        m_copy(w, 1).start()
-        m_copy(w, 3).start()
-        l_part(w, 0)
-
-    def l_start(w):
-        m_copy(w, 1).wait_recv()
-        n_copy(w, 0).start()
-        l_part(w, 1)
-        m_copy(w, 3).wait_recv()
-        n_copy(w, 1).start()
-        l_part(w, 3)
-
-    def l_finish(w):
-        n_copy(w, 0).wait_recv()
-        n_copy(w, 1).wait_recv()
-        l_part(w, 2)
-        d_copy(w, 0).start()
-
-    def f_start(w):
-        for part in (0, 1, 3, 2):
+    def m_start(*ws):
+        for w in ws:
+            seven = full[w].at[pl.ds(0, NZ - 1), c, :, mine(w, y)]
+            if w == 0:
+                await_bytes(seven, z_recv.at[w])
+            await_bytes(seven, z_send.at[w])
+            m_copy(w, 1).start()
+            m_copy(w, 3).start()
+        for w in ws:
+            l_part(w, 0)
+
+    def n_start(*ws):
+        for w in ws:
+            m_copy(w, 1).wait_recv()
+            n_copy(w, 0).start()
+            m_copy(w, 3).wait_recv()
+            n_copy(w, 1).start()
+
+    def l_start(*ws):
+        for w in ws:
+            l_part(w, 1)
+            l_part(w, 3)
+
+    def l_finish(*ws):
+        for w in ws:
+            n_copy(w, 0).wait_recv()
+            n_copy(w, 1).wait_recv()
+            l_part(w, 2)
+            d_copy(w, 0).start()
+
+    def f_part(w, *parts):
+        for part in parts:
             l_copy(w, 0, part).wait_recv()
             l_copy(w, 1, part).wait_recv()
             f_copy(w, part).start()
+
+    def f_finish(w, *parts):
+        f_part(w, *parts)
         d_copy(w, 1).start()
         d_copy(w, 3).start()
 
@@ -321,6 +338,7 @@
     rows_plus = plan_r[...].astype(f32) + 1.0
     drain_wave(1)
     send_wave(3)
+    n_start(0)
     l_start(0)
     ring_start(3)
     slot_ids = iota((64, 128), 1)
@@ -348,7 +366,9 @@
     other_rows = jnp.where(to_me, other_rows, -1)
     drain_wave(2)
     send_wave(4)
+    f_part(0, 0)
     l_finish(0)
+    f_part(0, 1)
     ring_start(4)
     back_cols = turned(back_rows)
     for n in range(ROWS // 128):
@@ -380,10 +400,9 @@
             same = q_cols[128 * a : 128 * (a + 1)] == keys
             bias[a, :, 128 * n : 128 * (n + 1)] = jnp.where(same, 0.0, -1e30)
 
-    f_start(0)
+    f_finish(0, 3, 2)
     ring_wait(4)
-    for w in rest:
-        m_start(w)
+    m_start(3, 1, 2)
     drain_wave(4)
     drain_wave(5)
     drain_wave(6)
@@ -397,8 +416,6 @@
         span = x_blocks(n)
         await_bytes(inbox.at[0, span], a_recv.at[n])
         remote(inbox.at[0, span], inbox.at[1, span], ad_send, ad_recv, partner).start()
-    for w in rest:
-        l_start(w)
     await_bytes(inbox.at[0], ad_send)
     await_bytes(inbox.at[1], ad_recv)
 
@@ -429,11 +446,12 @@
         )
 
     near_copy.start()
+    n_start(3, 1, 2)
     far_copy(0).start()
-    far_copy(1).start()
+    l_start(3, 1, 2)
 
     weights_done(0)
-    TILE = 256
+    TILE = 512
 
     def columns(rows, weight, start, count, store):
         def step(j, _):
@@ -471,12 +489,12 @@
     near_copy.wait()
     near = 2 * (1 - c)
     keys_values(normed[near], rows_at(near * ROWS, ROWS))
-    for w in rest:
-        l_finish(w)
+    l_finish(3, 1, 2)
+    far_copy(1).start()
 
     low_half = iota((128, 128), 1) < 64
 
-    def attend(n):
+    def attend(n, heads=(0, HEADS // 2)):
         a = jnp.where(c == 1, n, 2 - n)
         rows = rows_at(128 * a, 128)
         span = rows_at(128 * a, BAND)
@@ -499,14 +517,18 @@
             att[rows, part] = jnp.where(low_half, mixed[:128], mixed[128:]).astype(bf16)
             return 0
 
-        lax.fori_loop(0, HEADS // 2, step, 0)
+        lax.fori_loop(*heads, step, 0, unroll=4)
 
     far_keys(0)
     attend(0)
-    for w in rest:
-        f_start(w)
+    for w in (1, 2):
+        f_part(w, 0, 1, 3)
     far_keys(1)
-    attend(1)
+    for w in (1, 2):
+        f_finish(w, 2)
+    attend(1, (0, HEADS // 4))
+    f_finish(3, 0, 1, 3, 2)
+    attend(1, (HEADS // 4, HEADS // 2))
     last_start(1)
     attend(2)
     last_start(2)
@@ -563,6 +585,7 @@
         ).start()
         each(CHIPS, lambda i: r_copy(half, order(i)).start())
 
+    out_copies = []
     for half in range(2):
         part = slice(half * HALF, (half + 1) * HALF)
         cols = pl.ds(half * HALF, HALF)
@@ -574,28 +597,35 @@
                 rd_send.at[half], rd_recv.at[half], partner,
             ).start()
         await_bytes(home.at[1, :, :, cols], rd_recv.at[half])
-        out[:, part] = (
+        res[:, part] = (
             dot(pick_home[:, :SLOTS], home[0, :, :, part].reshape(SLOTS, HALF))
             + dot(pick_home[:, SLOTS:], home[1, :, :, part].reshape(SLOTS, HALF))
         ).astype(bf16)
+        cp = pltpu.make_async_copy(res.at[:, part], out.at[:, part], own_sem.at[half])
+        cp.start()
+        out_copies.append(cp)
     for half in range(2):
         cols = pl.ds(half * HALF, HALF)
         await_bytes(home.at[0, pl.ds(0, CHIPS - 1), :, cols], r_send.at[half])
         await_bytes(home.at[0, :, :, cols], rd_send.at[half])
     for w in range(4):
         weights_sent(w)
+    for cp in out_copies:
+        cp.wait()
 
 
 def local(tokens, modality, type_embed, dest_shard, dest_row, segments, w_qkv, w_out, w_up, w_down):
-    vmem = pl.BlockSpec(memory_space=pltpu.VMEM)
     dma = pltpu.SemaphoreType.DMA
     V = pltpu.VMEM
     result = pl.pallas_call(
         kernel,
         out_shape=jax.ShapeDtypeStruct((ROWS, WIDTH), bf16),
-        in_specs=[vmem] * 10,
-        out_specs=vmem,
+        in_specs=[pl.BlockSpec(memory_space=pltpu.HBM)] * 10,
+        out_specs=pl.BlockSpec(memory_space=pltpu.HBM),
         scratch_shapes=[
+            V((ROWS, WIDTH), bf16), V((1, ROWS), i32), V((2, WIDTH), bf16),
+            V((1, 64 * ROWS), i32), V((1, 64 * ROWS), i32), V((1, 64 * ROWS), i32),
+            dma((6,)), dma((4,)),
             V((CHIPS, 2, 16, 3 * WIDTH), bf16),
             V((CHIPS, 2, 16, WIDTH), bf16),
             V((CHIPS, 2, 16, FF), bf16),
@@ -626,7 +656,7 @@
             dma((3,)), dma((3,)),
         ],
         compiler_params=pltpu.CompilerParams(
-            collective_id=0, has_side_effects=True, vmem_limit_bytes=63 * 1024 * 1024
+            collective_id=0, has_side_effects=True, vmem_limit_bytes=58 * 1024 * 1024
         ),
         name="encoder",
     )(tokens[0], modality, type_embed, dest_shard, dest_row, segments, w_qkv, w_out, w_up, w_down)

time: 141 us -> 136 us (0.965)
  Pallas kernels: 139 us -> 133 us
    pallas_call x1, Pallas kernels: 139 us -> 133 us  [local(): pl.pallas_call(kernel, out_shape=jax.ShapeDtypeStruct((ROWS, WIDTH), bf16...]
where the time goes in v3:
time: 136 us; the launch traced here: 135 us
  Pallas kernels  133 us (98%)
  local copies, waits for them, and re-layouts  2.06 us (2%)
    pallas_call x1, Pallas kernels, local(): pl.pallas_call(kernel, out_shape=jax.ShapeDtypeStruct((ROWS, WIDTH), bf16...  133 us

profile of v3, /device:TPU:1, one launch (start us, length us, event | category | flops | bytes accessed | tf_op | source)
XLA Modules:
  0.0 135.5 jit_solution(3140255968646842708)
XLA Ops:
  0.0 133.4 %encoder.1 = bf16[384,1024]{1,0:T(8,128)(2,1)} custom-call(bf16[384,1024]{1,0:T(8,128)(2,1)} %bitcast.3, s32[1,384]{1,0:T(1,128)} %mod_in.1, bf16[2,1024]{1,0:T(2,128)(2,1)} %temb_in.1, s32[1,24576]{1,0:T(1,128)} %dsh_in.1, s32[1,24576]{1,0:T(1,128)} %drow_in.1, s32[1,24576]{1,0:T(1,128)} %seg_in.1, bf16[16,768]{1,0:T(8,128)(2,1)} %w_qkv.1, ...), custom_call_target="tpu_custom_call" | custom-call | tf_op jit(solution)/shard_map/encoder/pallas_call | solution.py:620
  133.4 2.1 %copy.12 = bf16[1,384,1024]{2,1,0:T(8,128)(2,1)} copy(bf16[1,384,1024]{2,1,0:T(8,128)(2,1)} %bitcast.2) | data formatting | bytes 1572864
